TPU v7x, 32 devices: a whole 2x2x4 slice. The times are simulated.
32 devices in a mesh: pipe: 4 (over x, core), vocab: 8 (over z, y).
Axes of the slice: x: 2, y: 2, z: 4, core: 2. Of those that a mesh axis runs over, the one named last changes fastest.
Arguments:
- hidden: bfloat16 [4, 128, 4096], P('pipe'), may hold values from -60 to 60
- norm_gain: float32 [4096], replicated, may hold values from 0.5 to 1.5
- out_weight: bfloat16 [128256, 4096], P(('pipe', 'vocab')), may hold values from -4 to 4
- targets: int32 [4, 128], P('pipe'), may hold values from 0 to 128255
- loss_mask: int32 [4, 128], P('pipe'), may hold values from 0 to 1, as said below
- slot_position: int32 [4, 128], P('pipe'), may hold values from 0 to 127, each once within a row
- counts: int32 [4], replicated, may hold values from 1 to 128, 320 in all
- loss_scale: float32 [], replicated, may hold values from 4096 to 32768
Outputs:
- loss: float32 [], replicated
- grad_hidden: bfloat16 [4, 128, 4096], P('pipe')
Inputs may be any that keep to these rules, and one draw needn't show every extreme that they name: The 4 counts sum to exactly 320, and one of them equals 128. Each row of slot_position holds every number of 0 to 127 once. Each row of loss_mask holds at least 64 ones.
All inputs are finite; a program needn't handle non-finite values.
Results may differ from a plain program's by a relative error of at most 0.0034.
Values may be sent and summed in bfloat16 or wider, within the bound.
A program may use at most 128 MiB of HBM per device.

v0:
```python
import jax
import jax.numpy as jnp
from jax import lax
from jax.sharding import PartitionSpec as P

EPSILON = 1e-05


def rms_scale(values, norm_gain):
    mean_square = jnp.mean(values * values, axis=-1, keepdims=True)
    return values * lax.rsqrt(mean_square + EPSILON) * norm_gain


def pull_rows(rows, norm_gain, cotangent):
    pullback = jax.vjp(lambda values: rms_scale(values, norm_gain), rows)[1]
    return pullback(cotangent)[0].astype(jnp.bfloat16)


def softmax_stats(logits, local_target):
    row_top = lax.pmax(jnp.max(logits, axis=1), ("pipe", "vocab"))
    local_total = jnp.sum(jnp.exp(logits - row_top[:, None]), axis=1)
    exp_total, target_logit = lax.psum((local_total, local_target), ("pipe", "vocab"))
    return (row_top + jnp.log(exp_total), target_logit)


def body(hidden, norm_gain, out_weight, targets, loss_mask, slot_position, counts, loss_scale):
    micro_slots = hidden.shape[1]
    model_width = hidden.shape[2]
    shard_words = out_weight.shape[0]
    offset = lax.axis_index(("pipe", "vocab")) * shard_words
    own_rows = hidden.reshape(micro_slots, model_width).astype(jnp.float32)
    own_normed = rms_scale(own_rows, norm_gain).astype(jnp.bfloat16)
    all_normed, all_targets, all_masks, all_positions = (
        lax.all_gather(own_normed, "pipe", axis=0, tiled=True),
        lax.all_gather(targets.reshape(micro_slots), "pipe", axis=0, tiled=True),
        lax.all_gather(loss_mask.reshape(micro_slots), "pipe", axis=0, tiled=True),
        lax.all_gather(slot_position.reshape(micro_slots), "pipe", axis=0, tiled=True),
    )
    rows_total = all_normed.shape[0]
    micro_index = jnp.arange(rows_total, dtype=jnp.int32) // micro_slots
    count_row = jnp.sum(
        jnp.where(
            micro_index[:, None] == jnp.arange(counts.shape[0], dtype=jnp.int32)[None, :],
            counts[None, :],
            0,
        ),
        axis=1,
    )
    inside = all_positions < count_row
    token_weight = jnp.where(inside & (all_masks == 1), 1.0, 0.0).astype(jnp.float32)
    weight_total = jnp.sum(token_weight)
    work_normed, work_targets, work_weight = (all_normed, all_targets, token_weight)
    logits = lax.dot_general(
        work_normed, out_weight, (((1,), (1,)), ((), ())), preferred_element_type=jnp.float32
    )
    is_target = (
        jnp.arange(shard_words, dtype=jnp.int32)[None, :] == (work_targets - offset)[:, None]
    )
    local_target = jnp.sum(jnp.where(is_target, logits, 0.0), axis=1)
    log_total, target_logit = softmax_stats(logits, local_target)
    loss = jnp.sum(work_weight * (log_total - target_logit)) / weight_total
    token_coef = loss_scale * work_weight / weight_total
    logit_grad = (
        (jnp.exp(logits - log_total[:, None]) - is_target.astype(jnp.float32)) * token_coef[:, None]
    ).astype(jnp.bfloat16)
    work_grad = jnp.dot(logit_grad, out_weight, preferred_element_type=jnp.float32)
    grad_cube = work_grad.reshape(rows_total // micro_slots, micro_slots, model_width)
    micro_grad = lax.psum_scatter(grad_cube, "pipe", scatter_dimension=0, tiled=True)
    summed = lax.psum(micro_grad, "vocab")
    grad_out = pull_rows(own_rows, norm_gain, summed.reshape(micro_slots, model_width))
    return (loss, grad_out.reshape(1, micro_slots, model_width))


def solution(mesh):
    in_specs = (
        P("pipe", None, None),
        P(),
        P(("pipe", "vocab"), None),
        P("pipe", None),
        P("pipe", None),
        P("pipe", None),
        P(),
        P(),
    )
    out_specs = (P(), P("pipe", None, None))
    return jax.shard_map(body, mesh=mesh, in_specs=in_specs, out_specs=out_specs, check_vma=False)
```

profile of v0, /device:TPU:0, one launch (start us, length us, event | category | flops | bytes accessed | tf_op | source)
XLA Modules:
  0.0 372.7 jit_solution(8846889576664135234)
XLA Ops:
  7.2 0.0 copy-start.3
  7.2 0.0 copy-start.4
  7.2 0.0 copy-start.5
  7.2 0.0 copy-start.6
  7.2 0.0 all-gather.5.cloned.1.call-start
  7.3 1.5 fusion.7
  8.8 2.5 fusion.9
  11.3 0.0 all-gather.5.cloned.1.call-update
  11.3 0.0 reduce-scatter.2.cloned.1.call-start
  12.0 0.0 copy-done.3
  12.0 6.0 %all-gather.2 = s32[1,512]{1,0:T(1,128)S(1)} all-gather(s32[1,128]{1,0:T(1,128)S(1)} %copy-done.3), channel_id=4, replica_groups=mesh['pipe'=4,'vocab'=8] {'pipe'}, dimensions={1}, use_global_device_ids=true | all-gather | bytes 2560 | tf_op jit(solution)/shard_map/all_gather | solution.py:35
  18.1 0.0 copy-done.4
  18.1 5.4 %all-gather.1 = s32[1,512]{1,0:T(1,128)S(1)} all-gather(s32[1,128]{1,0:T(1,128)S(1)} %copy-done.4), channel_id=3, replica_groups=mesh['pipe'=4,'vocab'=8] {'pipe'}, dimensions={1}, use_global_device_ids=true | all-gather | bytes 2560 | tf_op jit(solution)/shard_map/all_gather | solution.py:36
  23.4 0.0 copy-done.5
  23.4 5.2 %all-gather = s32[1,512]{1,0:T(1,128)S(1)} all-gather(s32[1,128]{1,0:T(1,128)S(1)} %copy-done.5), channel_id=2, replica_groups=mesh['pipe'=4,'vocab'=8] {'pipe'}, dimensions={1}, use_global_device_ids=true | all-gather | bytes 2560 | tf_op jit(solution)/shard_map/all_gather | solution.py:37
  28.6 0.0 copy-done.6
  28.6 0.1 select_reduce_fusion.1
  28.7 19.9 %all-gather.5.cloned.1.call-done = bf16[512,4096]{1,0:T(8,128)(2,1)} async-done(((bf16[128,4096]{1,0:T(8,128)(2,1)}), bf16[512,4096]{1,0:T(8,128)(2,1)}) %all-gather.5.cloned.1.call-update) | async-done | bytes 4194320 | tf_op jit(solution)/shard_map/all_gather | solution.py:34
  48.7 23.8 %fusion.18 = (f32[512]{0:T(512)S(1)}, f32[512,4008]{0,1:T(8,128)}) fusion(bf16[512,4096]{1,0:T(8,128)(2,1)} %all-gather.5.cloned.1.call-done, bf16[4008,4096]{1,0:T(8,128)(2,1)} %param.10), kind=kOutput, calls=%fused_computation.41 | convolution fusion | flops 16812822528 | bytes 45238272 | tf_op jit(solution)/shard_map/dot_general | solution.py:53
  72.4 39.2 %pmax.7 = f32[512]{0:T(512)S(1)} all-reduce(f32[512]{0:T(512)S(1)} %get-tuple-element.10), channel_id=1, replica_groups=mesh['pipe'=4,'vocab'=8] {'pipe','vocab'}, use_global_device_ids=true, to_apply=%region_3.4 | all-reduce | flops 512 | bytes 4096 | tf_op jit(solution)/shard_map/pmax | solution.py:20
  111.7 4.5 %select_reduce_fusion = (f32[512]{0:T(512)S(1)}, f32[512]{0:T(512)S(1)}) fusion(f32[512,4008]{0,1:T(8,128)} %get-tuple-element.11, s32[512]{0:T(512)S(1)} %bitcast.27, f32[512]{0:T(512)S(1)} %pmax.7), kind=kLoop, calls=%fused_computation.1 | loop fusion | flops 10259456 | bytes 8216576 | tf_op jit(solution)/shard_map/reduce_sum | solution.py:59
  116.2 41.0 %all-reduce = (f32[512]{0:T(512)S(1)}, f32[512]{0:T(512)S(1)}) all-reduce(f32[512]{0:T(512)S(1)} %get-tuple-element.3, f32[512]{0:T(512)S(1)} %get-tuple-element.2), channel_id=1, replica_groups=mesh['pipe'=4,'vocab'=8] {'pipe','vocab'}, use_global_device_ids=true, to_apply=%region_5.6 | all-reduce | flops 1024 | bytes 8192 | tf_op jit(solution)/shard_map/psum | solution.py:22
  157.1 0.6 select_reduce_fusion.2
  157.8 0.7 fusion.13
  158.4 25.5 %fusion = f32[512,4096]{1,0:T(8,128)} fusion(bf16[4008,4096]{1,0:T(8,128)(2,1)} %param.10, f32[512,4008]{0,1:T(8,128)} %get-tuple-element.11, f32[512]{0:T(512)S(1)} %fusion.13, f32[512]{0:T(512)S(1)} %get-tuple-element.8, s32[512]{0:T(512)S(1)} %bitcast.28), kind=kOutput, calls=%fused_computation.4 | convolution fusion | flops 16823083008 | bytes 49436672 | tf_op jit(solution)/shard_map/dot_general | solution.py:66
  183.9 0.0 copy-start
  183.9 0.0 copy-start.2
  183.9 0.0 reduce-scatter.2.cloned.1.call-update
  184.0 0.0 all-reduce.3.cloned.1.call-start
  184.0 71.2 %reduce-scatter.2.cloned.1.call-done = f32[1,128,4096]{2,1,0:T(8,128)} async-done(((f32[4,128,4096]{2,1,0:T(8,128)}), f32[1,128,4096]{2,1,0:T(8,128)}) %reduce-scatter.2.cloned.1.call-update) | async-done | bytes 2097168 | tf_op jit(solution)/shard_map/reduce_scatter | solution.py:68
  255.3 0.0 all-reduce.3.cloned.1.call-update
  256.6 104.7 %all-reduce.3.cloned.1.call-done = f32[1,128,4096]{2,1,0:T(8,128)} async-done(((f32[1,128,4096]{2,1,0:T(8,128)}), f32[1,128,4096]{2,1,0:T(8,128)}) %all-reduce.3.cloned.1.call-update) | async-done | bytes 2097168 | tf_op jit(solution)/shard_map/psum | solution.py:69
  361.3 0.0 copy-done
  361.3 0.0 copy-done.2
  361.3 0.0 copy-start.1
  361.3 2.1 fusion.10
  363.4 0.1 copy-done.1
  363.5 1.5 fusion.11
  (5 shorter events, 0.0 us)
Async XLA Ops:
  7.2 4.9 %copy-start.3 = (s32[1,128]{1,0:T(1,128)S(1)}, s32[1,128]{1,0:T(1,128)}, u32[]{:S(2)}) copy-start(s32[1,128]{1,0:T(1,128)} %param.11) | copy-start | bytes 1540
  7.2 10.9 %copy-start.4 = (s32[1,128]{1,0:T(1,128)S(1)}, s32[1,128]{1,0:T(1,128)}, u32[]{:S(2)}) copy-start(s32[1,128]{1,0:T(1,128)} %param.12) | copy-start | bytes 1540
  7.2 16.2 %copy-start.5 = (s32[1,128]{1,0:T(1,128)S(1)}, s32[1,128]{1,0:T(1,128)}, u32[]{:S(2)}) copy-start(s32[1,128]{1,0:T(1,128)} %param.13) | copy-start | bytes 1540
  7.2 21.4 %copy-start.6 = (s32[4]{0:T(128)S(1)}, s32[4]{0:T(128)}, u32[]{:S(2)}) copy-start(s32[4]{0:T(128)} %param.14) | copy-start | bytes 52
  7.2 41.5 %all-gather.5.cloned.1.call-start = ((), (), s32[]{:S(2)}) async-start(), calls=%async_computation.1 | async-start | bytes 5242880 | tf_op jit(solution)/shard_map/all_gather | solution.py:34
  11.3 243.9 %reduce-scatter.2.cloned.1.call-start = ((), (), s32[]{:S(2)}) async-start(), calls=%async_computation.2 | async-start | bytes 10485760 | tf_op jit(solution)/shard_map/reduce_scatter | solution.py:68
  183.9 177.3 %copy-start = (bf16[1,128,4096]{2,1,0:T(8,128)(2,1)S(1)}, bf16[1,128,4096]{2,1,0:T(8,128)(2,1)}, u32[]{:S(2)}) copy-start(bf16[1,128,4096]{2,1,0:T(8,128)(2,1)} %param.8) | copy-start | bytes 3145732
  183.9 177.3 %copy-start.2 = (f32[4096]{0:T(1024)S(1)}, f32[4096]{0:T(1024)}, u32[]{:S(2)}) copy-start(f32[4096]{0:T(1024)} %param.9) | copy-start | bytes 49156
  184.0 177.3 %all-reduce.3.cloned.1.call-start = ((), (), s32[]{:S(2)}) async-start(), calls=%async_computation.3 | async-start | bytes 4194304 | tf_op jit(solution)/shard_map/psum | solution.py:69
  361.3 2.2 copy-start.1
Sparse Core Ops, SparseCore 0:
  11.5 37.1 all-gather.4
  184.1 71.1 reduce-scatter.1
  258.9 102.3 all-reduce.2
where the time goes:
time: 373 us
  waiting for transfers between devices  196 us (53%)
  blocking collectives  96.8 us (26%)
  matrix products  49.3 us (13%)
  between operations  16.9 us (5%)
  other arithmetic  13.6 us (4%)
    psum x1, waiting for transfers between devices, body(): summed = lax.psum(micro_grad, 'vocab')  105 us
    reduce_scatter x1, waiting for transfers between devices, body(): lax.psum_scatter(grad_cube, 'pipe', scatter_dimension=0, tiled=True)  71.2 us
    psum x1, blocking collectives, softmax_stats(): lax.psum((local_total, local_target), ('pipe', 'vocab'))  41 us
    pmax x1, blocking collectives, softmax_stats(): row_top = lax.pmax(jnp.max(logits, axis=1), ('pipe', 'vocab'))  39.2 us
    dot_general x1, matrix products, body(): jnp.dot(logit_grad, out_weight, preferred_element_type=jnp.float32)  25.5 us
    dot_general x1, matrix products, body(): lax.dot_general(work_normed, out_weight, (((1,), (1,)), ((), ())), prefer...  23.8 us
    all_gather x1, waiting for transfers between devices, body(): lax.all_gather(own_normed, 'pipe', axis=0, tiled=True)  19.9 us
  transfers between devices with their start and end apart: 3, of which 3 were waited for; matrix products, arithmetic and copies ran while one was open for 0% of the time, Pallas kernels for 0%

commit v1 on v0

--- a/solution.py
+++ b/solution.py
@@ -66,7 +66,11 @@
     work_grad = jnp.dot(logit_grad, out_weight, preferred_element_type=jnp.float32)
     grad_cube = work_grad.reshape(rows_total // micro_slots, micro_slots, model_width)
     micro_grad = lax.psum_scatter(grad_cube, "pipe", scatter_dimension=0, tiled=True)
-    summed = lax.psum(micro_grad, "vocab")
+    size = lax.axis_size("vocab")
+    summed, hop = (micro_grad, 1)
+    while hop < size:
+        summed = summed + lax.ppermute(summed, "vocab", [(i, i ^ hop) for i in range(size)])
+        hop = 2 * hop
     grad_out = pull_rows(own_rows, norm_gain, summed.reshape(micro_slots, model_width))
     return (loss, grad_out.reshape(1, micro_slots, model_width))
 

time: 373 us -> 457 us (1.23)
  waiting for transfers between devices: 196 us -> 270 us
  starting transfers between devices: 0.12 us -> 5.62 us
    ppermute x0 -> x3, waiting for transfers between devices: none -> 178 us  [body(): lax.ppermute(summed, 'vocab', [(i, i ^ hop) for i in range(size)])]
    psum x1 -> x0, waiting for transfers between devices: 105 us -> none  [body(): summed = lax.psum(micro_grad, 'vocab')]
    ppermute x0 -> x3, starting transfers between devices: none -> 5.54 us  [body(): lax.ppermute(summed, 'vocab', [(i, i ^ hop) for i in range(size)])]
  transfers between devices with their start and end apart: 3 -> 5, of which waited for: 3 -> 5; matrix products, arithmetic and copies ran while one was open for 0% -> 0% of each run, Pallas kernels for 0% -> 0%
where the time goes in v1:
time: 457 us; the launch traced here: 456 us
  waiting for transfers between devices  270 us (59%)
  blocking collectives  96.9 us (21%)
  matrix products  49.3 us (11%)
  other arithmetic  17.4 us (4%)
  between operations  17.3 us (4%)
  starting transfers between devices  5.62 us (1%)
    ppermute x3, waiting for transfers between devices, body(): lax.ppermute(summed, 'vocab', [(i, i ^ hop) for i in range(size)])  178 us
    reduce_scatter x1, waiting for transfers between devices, body(): lax.psum_scatter(grad_cube, 'pipe', scatter_dimension=0, tiled=True)  71.4 us
    psum x1, blocking collectives, softmax_stats(): lax.psum((local_total, local_target), ('pipe', 'vocab'))  41.1 us
    pmax x1, blocking collectives, softmax_stats(): row_top = lax.pmax(jnp.max(logits, axis=1), ('pipe', 'vocab'))  39.2 us
    dot_general x1, matrix products, body(): jnp.dot(logit_grad, out_weight, preferred_element_type=jnp.float32)  25.5 us
    dot_general x1, matrix products, body(): lax.dot_general(work_normed, out_weight, (((1,), (1,)), ((), ())), prefer...  23.7 us
    all_gather x1, waiting for transfers between devices, body(): lax.all_gather(own_normed, 'pipe', axis=0, tiled=True)  19.9 us
  transfers between devices with their start and end apart: 5, of which 5 were waited for; matrix products, arithmetic and copies ran while one was open for 0% of the time, Pallas kernels for 0%

profile of v1, /device:TPU:0, one launch (start us, length us, event | category | flops | bytes accessed | tf_op | source)
XLA Modules:
  0.0 456.2 jit_solution(1102869830318089280)
XLA Ops:
  7.2 0.0 copy-start.2
  7.2 0.0 copy-start.3
  7.2 0.0 copy-start.4
  7.2 0.0 copy-start.5
  7.2 0.0 all-gather.5.cloned.1.call-start
  7.3 1.5 fusion.7
  8.8 2.5 fusion.9
  11.3 0.0 all-gather.5.cloned.1.call-update
  11.3 0.0 reduce-scatter.2.cloned.1.call-start
  12.0 0.0 copy-done.2
  12.0 6.0 %all-gather.2 = s32[1,512]{1,0:T(1,128)S(1)} all-gather(s32[1,128]{1,0:T(1,128)S(1)} %copy-done.2), channel_id=4, replica_groups=mesh['pipe'=4,'vocab'=8] {'pipe'}, dimensions={1}, use_global_device_ids=true | all-gather | bytes 2560 | tf_op jit(solution)/shard_map/all_gather | solution.py:35
  18.1 0.0 copy-done.3
  18.1 5.4 %all-gather.1 = s32[1,512]{1,0:T(1,128)S(1)} all-gather(s32[1,128]{1,0:T(1,128)S(1)} %copy-done.3), channel_id=3, replica_groups=mesh['pipe'=4,'vocab'=8] {'pipe'}, dimensions={1}, use_global_device_ids=true | all-gather | bytes 2560 | tf_op jit(solution)/shard_map/all_gather | solution.py:36
  23.4 0.0 copy-done.4
  23.4 5.2 %all-gather = s32[1,512]{1,0:T(1,128)S(1)} all-gather(s32[1,128]{1,0:T(1,128)S(1)} %copy-done.4), channel_id=2, replica_groups=mesh['pipe'=4,'vocab'=8] {'pipe'}, dimensions={1}, use_global_device_ids=true | all-gather | bytes 2560 | tf_op jit(solution)/shard_map/all_gather | solution.py:37
  28.6 0.0 copy-done.5
  28.6 0.1 select_reduce_fusion.1
  28.7 19.9 %all-gather.5.cloned.1.call-done = bf16[512,4096]{1,0:T(8,128)(2,1)} async-done(((bf16[128,4096]{1,0:T(8,128)(2,1)}), bf16[512,4096]{1,0:T(8,128)(2,1)}) %all-gather.5.cloned.1.call-update) | async-done | bytes 4194320 | tf_op jit(solution)/shard_map/all_gather | solution.py:34
  48.7 23.7 %fusion.18 = (f32[512]{0:T(512)S(1)}, f32[512,4008]{0,1:T(8,128)}) fusion(bf16[512,4096]{1,0:T(8,128)(2,1)} %all-gather.5.cloned.1.call-done, bf16[4008,4096]{1,0:T(8,128)(2,1)} %param.10), kind=kOutput, calls=%fused_computation.41 | convolution fusion | flops 16812822528 | bytes 45238272 | tf_op jit(solution)/shard_map/dot_general | solution.py:53
  72.4 39.2 %pmax.7 = f32[512]{0:T(512)S(1)} all-reduce(f32[512]{0:T(512)S(1)} %get-tuple-element.10), channel_id=1, replica_groups=mesh['pipe'=4,'vocab'=8] {'pipe','vocab'}, use_global_device_ids=true, to_apply=%region_3.4 | all-reduce | flops 512 | bytes 4096 | tf_op jit(solution)/shard_map/pmax | solution.py:20
  111.7 4.5 select_reduce_fusion
  116.2 41.1 %all-reduce = (f32[512]{0:T(512)S(1)}, f32[512]{0:T(512)S(1)}) all-reduce(f32[512]{0:T(512)S(1)} %get-tuple-element.3, f32[512]{0:T(512)S(1)} %get-tuple-element.2), channel_id=1, replica_groups=mesh['pipe'=4,'vocab'=8] {'pipe','vocab'}, use_global_device_ids=true, to_apply=%region_5.6 | all-reduce | flops 1024 | bytes 8192 | tf_op jit(solution)/shard_map/psum | solution.py:22
  157.3 0.6 select_reduce_fusion.2
  157.9 0.7 fusion.13
  158.5 25.5 %fusion = f32[512,4096]{1,0:T(8,128)} fusion(bf16[4008,4096]{1,0:T(8,128)(2,1)} %param.10, f32[512,4008]{0,1:T(8,128)} %get-tuple-element.11, f32[512]{0:T(512)S(1)} %fusion.13, f32[512]{0:T(512)S(1)} %get-tuple-element.8, s32[512]{0:T(512)S(1)} %bitcast.28), kind=kOutput, calls=%fused_computation.4 | convolution fusion | flops 16823083008 | bytes 49436672 | tf_op jit(solution)/shard_map/dot_general | solution.py:66
  184.1 0.0 reduce-scatter.2.cloned.1.call-update
  184.1 71.4 %reduce-scatter.2.cloned.1.call-done = f32[1,128,4096]{2,1,0:T(8,128)} async-done(((f32[4,128,4096]{2,1,0:T(8,128)}), f32[1,128,4096]{2,1,0:T(8,128)}) %reduce-scatter.2.cloned.1.call-update) | async-done | bytes 2097168 | tf_op jit(solution)/shard_map/reduce_scatter | solution.py:68
  255.5 1.5 collective-permute-start
  256.9 45.9 %collective-permute-done = f32[1,128,4096]{2,1,0:T(8,128)S(1)} collective-permute-done((f32[1,128,4096]{2,1,0:T(8,128)}, f32[1,128,4096]{2,1,0:T(8,128)S(1)}, u32[]{:S(2)}, u32[]{:S(2)}) %collective-permute-start) | collective-permute-done | bytes 2097184 | tf_op jit(solution)/shard_map/ppermute | solution.py:72
  302.9 1.8 add.40
  304.7 0.0 copy-start
  304.7 0.0 copy-start.1
  304.7 1.5 collective-permute-start.1
  306.3 44.9 %collective-permute-done.1 = f32[1,128,4096]{2,1,0:T(8,128)S(1)} collective-permute-done((f32[1,128,4096]{2,1,0:T(8,128)S(1)}, f32[1,128,4096]{2,1,0:T(8,128)S(1)}, u32[]{:S(2)}, u32[]{:S(2)}) %collective-permute-start.1) | collective-permute-done | bytes 2097184 | tf_op jit(solution)/shard_map/ppermute | solution.py:72
  351.1 0.2 add.41
  351.4 2.5 collective-permute-start.2
  355.2 87.6 %collective-permute-done.2 = f32[1,128,4096]{2,1,0:T(8,128)} collective-permute-done((f32[1,128,4096]{2,1,0:T(8,128)S(1)}, f32[1,128,4096]{2,1,0:T(8,128)}, u32[]{:S(2)}, u32[]{:S(2)}) %collective-permute-start.2) | collective-permute-done | bytes 2097184 | tf_op jit(solution)/shard_map/ppermute | solution.py:72
  442.9 0.0 copy-done
  442.9 0.0 copy-done.1
  442.9 2.1 fusion.10
  445.0 3.3 fusion.11
  (5 shorter events, 0.0 us)
Async XLA Ops:
  7.2 4.9 %copy-start.2 = (s32[1,128]{1,0:T(1,128)S(1)}, s32[1,128]{1,0:T(1,128)}, u32[]{:S(2)}) copy-start(s32[1,128]{1,0:T(1,128)} %param.11) | copy-start | bytes 1540
  7.2 10.9 %copy-start.3 = (s32[1,128]{1,0:T(1,128)S(1)}, s32[1,128]{1,0:T(1,128)}, u32[]{:S(2)}) copy-start(s32[1,128]{1,0:T(1,128)} %param.12) | copy-start | bytes 1540
  7.2 16.2 %copy-start.4 = (s32[1,128]{1,0:T(1,128)S(1)}, s32[1,128]{1,0:T(1,128)}, u32[]{:S(2)}) copy-start(s32[1,128]{1,0:T(1,128)} %param.13) | copy-start | bytes 1540
  7.2 21.4 %copy-start.5 = (s32[4]{0:T(128)S(1)}, s32[4]{0:T(128)}, u32[]{:S(2)}) copy-start(s32[4]{0:T(128)} %param.14) | copy-start | bytes 52
  7.2 41.5 %all-gather.5.cloned.1.call-start = ((), (), s32[]{:S(2)}) async-start(), calls=%async_computation.1 | async-start | bytes 5242880 | tf_op jit(solution)/shard_map/all_gather | solution.py:34
  11.3 244.1 %reduce-scatter.2.cloned.1.call-start = ((), (), s32[]{:S(2)}) async-start(), calls=%async_computation.2 | async-start | bytes 10485760 | tf_op jit(solution)/shard_map/reduce_scatter | solution.py:68
  255.5 47.4 %collective-permute-start = (f32[1,128,4096]{2,1,0:T(8,128)}, f32[1,128,4096]{2,1,0:T(8,128)S(1)}, u32[]{:S(2)}, u32[]{:S(2)}) collective-permute-start(f32[1,128,4096]{2,1,0:T(8,128)} %reduce-scatter.2.cloned.1.call-done), channel_id=1, source_target_pairs={{0,1},{1,0},{2,3},{3,2},{4,5},{5,4},{6,7},{7,6},{8,9},{9,8},{10,11... | collective-permute-start | bytes 6291464 | tf_op jit(solution)/shard_map/ppermute | solution.py:72
  304.7 138.2 %copy-start = (bf16[1,128,4096]{2,1,0:T(8,128)(2,1)S(1)}, bf16[1,128,4096]{2,1,0:T(8,128)(2,1)}, u32[]{:S(2)}) copy-start(bf16[1,128,4096]{2,1,0:T(8,128)(2,1)} %param.8) | copy-start | bytes 3145732
  304.7 138.2 %copy-start.1 = (f32[4096]{0:T(1024)S(1)}, f32[4096]{0:T(1024)}, u32[]{:S(2)}) copy-start(f32[4096]{0:T(1024)} %param.9) | copy-start | bytes 49156
  304.7 46.4 %collective-permute-start.1 = (f32[1,128,4096]{2,1,0:T(8,128)S(1)}, f32[1,128,4096]{2,1,0:T(8,128)S(1)}, u32[]{:S(2)}, u32[]{:S(2)}) collective-permute-start(f32[1,128,4096]{2,1,0:T(8,128)S(1)} %add.40), channel_id=1, source_target_pairs={{0,2},{1,3},{2,0},{3,1},{4,6},{5,7},{6,4},{7,5},{8,10},{9,11},{10,... | collective-permute-start | bytes 6291464 | tf_op jit(solution)/shard_map/ppermute | solution.py:72
  351.4 91.5 %collective-permute-start.2 = (f32[1,128,4096]{2,1,0:T(8,128)S(1)}, f32[1,128,4096]{2,1,0:T(8,128)}, u32[]{:S(2)}, u32[]{:S(2)}) collective-permute-start(f32[1,128,4096]{2,1,0:T(8,128)S(1)} %add.41), channel_id=1, source_target_pairs={{0,4},{1,5},{2,6},{3,7},{4,0},{5,1},{6,2},{7,3},{8,12},{9,13},{10,... | collective-permute-start | bytes 6291464 | tf_op jit(solution)/shard_map/ppermute | solution.py:72
Sparse Core Ops, SparseCore 0:
  11.5 37.1 all-gather.4
  184.2 71.1 reduce-scatter.1
